TPU v7x, 256 devices: a whole 4x4x8 slice. The times are simulated.
256 devices in a mesh: row: 8 (over x, core), col: 4 (over y), depth: 8 (over z).
Axes of the slice: x: 4, y: 4, z: 8, core: 2. Of those that a mesh axis runs over, the one named last changes fastest.
Arguments:
- left_values: bfloat16 [384, 32, 4, 529], P('row', ('col', 'depth')), may hold values from -1.25 to 1.25
- left_columns: int32 [384, 32, 4], P('row', ('col', 'depth')), may hold values from 0 to 39, as said below
- right_values: bfloat16 [32, 40, 4, 3, 529], P(('col', 'depth'), 'row'), may hold values from -1.75 to 1.75
- right_columns: int32 [32, 40, 4, 3], P(('col', 'depth'), 'row'), may hold values from 0 to 31, as said below
Outputs:
- product_matrix: bfloat16 [8832, 2944], P('row', ('col', 'depth'))
Inputs may be any that keep to these rules, and one draw needn't show every extreme that they name: `left_columns`: within one block row and panel the 4 entries are distinct. `right_columns`: within one block row and column tile the 3 entries are distinct.
All inputs are finite; a program needn't handle non-finite values.
Results may differ from a plain program's by a relative error of at most 0.001.
Values may be sent and summed in bfloat16 or wider, within the bound.
A program may use at most 128 MiB of HBM per device.

v0:
```python
import math

import jax
import jax.numpy as jnp
from jax import lax
from jax.sharding import PartitionSpec as P

PANEL = 40
CTW = 32


def in_one_piece(arrays, axis, dim, along):
    widths = [math.prod(a.shape[along:]) for a in arrays]
    both = jnp.concatenate(
        [a.reshape(*a.shape[:along], w) for a, w in zip(arrays, widths)], axis=along
    )
    whole = lax.all_gather(both, axis, axis=dim, tiled=True)
    pieces = jnp.split(whole, [sum(widths[:k]) for k in range(1, len(widths))], axis=along)
    return tuple(
        (b.reshape(*whole.shape[:along], *a.shape[along:]) for a, b in zip(arrays, pieces))
    )


def dense_left(values, columns, panel_width):
    rows_here, panels, slots, square = values.shape
    block_edge = math.isqrt(square)
    onehot = (
        columns.astype(jnp.float32)[..., None] == jnp.arange(panel_width, dtype=jnp.float32)
    ).astype(jnp.bfloat16)
    blocks = values.reshape(rows_here, panels, slots, block_edge, block_edge)
    filled = jnp.einsum(
        "mqsp,mqsab->qmapb", onehot, blocks, preferred_element_type=jnp.float32
    ).astype(jnp.bfloat16)
    return filled.reshape(panels, rows_here * block_edge, panel_width * block_edge)


def dense_right(values, columns, tile_width):
    panels, rows_here, tiles, slots, square = values.shape
    block_edge = math.isqrt(square)
    onehot = (
        columns.astype(jnp.float32)[..., None] == jnp.arange(tile_width, dtype=jnp.float32)
    ).astype(jnp.bfloat16)
    blocks = values.reshape(panels, rows_here, tiles, slots, block_edge, block_edge)
    filled = jnp.einsum(
        "qrtuc,qrtuab->qratcb", onehot, blocks, preferred_element_type=jnp.float32
    ).astype(jnp.bfloat16)
    return filled.reshape(panels, rows_here * block_edge, tiles * tile_width * block_edge)


def contract(left_values, left_codes, right_values, right_codes):
    left_filled = dense_left(left_values, left_codes, PANEL)
    pieces = in_one_piece((right_values, right_codes), "row", 1, 4)
    right_filled = dense_right(pieces[0], pieces[1], CTW)
    return jnp.einsum("qmk,qkn->mn", left_filled, right_filled, preferred_element_type=jnp.float32)


def body(left_values, left_columns, right_values, right_columns):
    right_codes = right_columns.astype(jnp.bfloat16)
    partial_sums = contract(left_values, left_columns, right_values, right_codes)
    result = lax.psum_scatter(partial_sums, ("col", "depth"), scatter_dimension=1, tiled=True)
    return result.astype(jnp.bfloat16)


def solution(mesh):
    placed = (
        P("row", ("col", "depth"), None, None),
        P("row", ("col", "depth"), None),
        P(("col", "depth"), "row", None, None, None),
        P(("col", "depth"), "row", None, None),
    )
    return jax.shard_map(
        body, mesh=mesh, in_specs=placed, out_specs=P("row", ("col", "depth")), check_vma=False
    )
```

profile of v0, /device:TPU:56, one launch (start us, length us, event | category | flops | bytes accessed | tf_op | source)
XLA Modules:
  0.0 356.1 jit_solution(7815934439125300105)
XLA Ops:
  0.0 0.7 convert_bitcast_fusion.1
  0.7 0.2 copy.35
  0.9 1.0 pad_maximum_fusion
  1.8 13.6 %all_gather.3 = bf16[1,40,4,3,530]{4,2,3,0,1:T(4,128)(2,1)S(1)} all-gather(bf16[1,5,4,3,530]{4,2,3,0,1:T(4,128)(2,1)S(1)} %pad_maximum_fusion), channel_id=1, replica_groups=mesh['row'=8,'col'=4,'depth'=8] {'row'}, dimensions={1}, use_global_device_ids=true | all-gather | bytes 572400 | tf_op jit(solution)/shard_map/all_gather | solution.py:17
  15.4 0.1 split.9
  15.5 1.2 copy.36
  16.8 6.2 %copy.39 = bf16[40,4,3,23,23]{4,2,3,1,0:T(4,128)(2,1)} copy(bf16[40,4,3,23,23]{0,1,4,3,2:T(4,128)(2,1)S(1)} %bitcast.44) | data formatting | bytes 1015680 | tf_op jit(solution)/shard_map/reshape.13
  23.0 0.2 copy.43
  23.2 0.1 copy.38
  23.3 17.1 %convert_bitcast_fusion = bf16[1,40,23,4,32,23]{4,5,2,3,1,0:T(8,128)(2,1)} fusion(bf16[40,4,3,23,23]{4,2,3,1,0:T(4,128)(2,1)} %copy.39, f32[40,4,3]{2,1,0:T(4,128)S(1)} %copy.38), kind=kOutput, calls=%fused_computation | convolution fusion | flops 18974720 | bytes 5926720 | tf_op jit(solution)/shard_map/qrtuc,qrtuab->qratcb/dot_general | solution.py:44
  40.4 41.1 %copy.40 = bf16[1,40,23,4,32,23]{5,4,3,2,1,0:T(8,128)(2,1)} copy(bf16[1,40,23,4,32,23]{4,5,2,3,1,0:T(8,128)(2,1)} %convert_bitcast_fusion) | data formatting | bytes 10833920 | tf_op jit(solution)/shard_map/convert_element_type | solution.py:46
  81.5 0.0 copy-start
  81.5 0.0 copy-start.1
  81.5 36.1 %reshape.47 = bf16[920,2944]{1,0:T(8,128)(2,1)} reshape(bf16[1,40,23,4,32,23]{5,4,3,2,1,0:T(8,128)(2,1)} %copy.40) | data formatting | bytes 10833920 | tf_op jit(solution)/shard_map/reshape.17
  117.7 0.0 copy-done
  117.7 0.9 copy.31
  118.6 3.5 copy.32
  122.0 0.0 copy-done.1
  122.0 0.1 copy.30
  122.1 5.7 %fusion.1 = bf16[1,48,23,40,23]{3,4,2,1,0:T(8,128)(2,1)} fusion(bf16[48,4,23,23]{3,1,2,0:T(4,128)(2,1)S(1)} %copy.32, f32[48,4]{1,0:T(8,128)S(1)} %copy.30), kind=kOutput, calls=%fused_computation.2 | convolution fusion | flops 9148800 | bytes 2235264 | tf_op jit(solution)/shard_map/mqsp,mqsab->qmapb/dot_general | solution.py:31
  127.9 23.6 %copy.33 = bf16[1,48,23,40,23]{2,1,4,3,0:T(8,128)(2,1)} copy(bf16[1,48,23,40,23]{3,4,2,1,0:T(8,128)(2,1)} %fusion.1) | data formatting | bytes 4062720 | tf_op jit(solution)/shard_map/convert_element_type | solution.py:33
  151.5 13.4 %reshape.44 = bf16[1104,920]{0,1:T(8,128)(2,1)S(1)} reshape(bf16[1,48,23,40,23]{2,1,4,3,0:T(8,128)(2,1)} %copy.33) | data formatting | bytes 4062720 | tf_op jit(solution)/shard_map/reshape.16
  164.9 13.3 %fusion.8 = f32[1104,2944]{0,1:T(8,128)} fusion(bf16[1104,920]{0,1:T(8,128)(2,1)S(1)} %reshape.44, bf16[920,2944]{1,0:T(8,128)(2,1)} %reshape.47), kind=kOutput, calls=%fused_computation.14 | convolution fusion | flops 5980323840 | bytes 20449024 | tf_op jit(solution)/shard_map/qmk,qkn->mn/dot_general | solution.py:54
  178.2 0.0 copy-start.2
  178.2 162.1 %fusion = f32[1104,96]{0,1:T(8,128)S(1)} fusion(f32[1104,2944]{0,1:T(8,128)} %fusion.8), kind=kCustom, calls=%all-reduce-scatter | all-reduce-scatter fusion | flops 3391489 | bytes 13425664
  340.3 1.9 collective-permute-start
  342.3 5.4 %collective-permute-start.1 = (bf16[1104,28]{0,1:T(8,128)(2,1)S(1)}, bf16[1104,28]{0,1:T(8,128)(2,1)S(1)}, u32[]{:S(2)}, u32[]{:S(2)}) collective-permute-start(bf16[1104,28]{0,1:T(8,128)(2,1)S(1)} %slice), channel_id=1, source_target_pairs={{0,2},{1,3},{2,4},{3,5},{4,6},{5,7},{6,8},{7,9},{8,10},{9,11},{10,... | collective-permute-start | bytes 185480
  347.7 0.0 copy-done.2
  347.7 0.6 dynamic-slice.4
  348.9 5.6 %collective-permute-done.1 = bf16[1104,28]{0,1:T(8,128)(2,1)S(1)} collective-permute-done((bf16[1104,28]{0,1:T(8,128)(2,1)S(1)}, bf16[1104,28]{0,1:T(8,128)(2,1)S(1)}, u32[]{:S(2)}, u32[]{:S(2)}) %collective-permute-start.1) | collective-permute-done | bytes 61856
  354.5 0.0 collective-permute-done
  354.5 0.8 concatenate.4
  355.3 0.7 dynamic-slice_convert_fusion
  (4 shorter events, 0.1 us)
Async XLA Ops:
  81.5 36.2 %copy-start = (bf16[48,1,4,529]{3,2,1,0:T(4,128)(2,1)S(1)}, bf16[48,1,4,529]{3,2,1,0:T(4,128)(2,1)}, u32[]{:S(2)}) copy-start(bf16[48,1,4,529]{3,2,1,0:T(4,128)(2,1)} %param.4) | copy-start | bytes 609412
  81.5 40.5 %copy-start.1 = (s32[48,1,4]{0,2,1:T(4,128)S(1)}, s32[48,1,4]{0,2,1:T(4,128)}, u32[]{:S(2)}) copy-start(s32[48,1,4]{0,2,1:T(4,128)} %param.5) | copy-start | bytes 2308
  178.2 169.5 %copy-start.2 = (u32[256]{0:T(256)S(1)}, u32[256]{0:T(256)}, u32[]{:S(2)}) copy-start(u32[256]{0:T(256)} %constant.6) | copy-start | bytes 3076
  340.3 14.2 %collective-permute-start = (bf16[1104,96]{0,1:T(8,128)(2,1)S(1)}, bf16[1104,96]{0,1:T(8,128)(2,1)S(1)}, u32[]{:S(2)}, u32[]{:S(2)}) collective-permute-start(bf16[1104,96]{0,1:T(8,128)(2,1)S(1)} %convert.3), channel_id=1, source_target_pairs={{0,1},{1,2},{2,3},{3,4},{4,5},{5,6},{6,7},{7,8},{8,9},{9,10},{10,1... | collective-permute-start | bytes 635912
  342.3 12.2 %collective-permute-start.1 = (bf16[1104,28]{0,1:T(8,128)(2,1)S(1)}, bf16[1104,28]{0,1:T(8,128)(2,1)S(1)}, u32[]{:S(2)}, u32[]{:S(2)}) collective-permute-start(bf16[1104,28]{0,1:T(8,128)(2,1)S(1)} %slice), channel_id=1, source_target_pairs={{0,2},{1,3},{2,4},{3,5},{4,6},{5,7},{6,8},{7,9},{8,10},{9,11},{10,... | collective-permute-start | bytes 185480
where the time goes:
time: 359 us; the launch traced here: 356 us
  blocking collectives  176 us (49%)
  local copies, waits for them, and re-layouts  129 us (36%)
  matrix products  36.2 us (10%)
  starting transfers between devices  7.32 us (2%)
  waiting for transfers between devices  5.56 us (2%)
    unnamed x1, blocking collectives  162 us
    another operation x4, local copies, waits for them, and re-layouts  59.2 us
    convert_element_type x1, local copies, waits for them, and re-layouts, dense_right(): filled = jnp.einsum('qrtuc,qrtuab->qratcb', onehot, blocks, preferred_ele...  41.1 us
    convert_element_type x1, local copies, waits for them, and re-layouts, dense_left(): filled = jnp.einsum('mqsp,mqsab->qmapb', onehot, blocks, preferred_elemen...  23.6 us
    dot_general x1, matrix products, dense_right(): jnp.einsum('qrtuc,qrtuab->qratcb', onehot, blocks, preferred_element_type...  17.1 us
    all_gather x1, blocking collectives, in_one_piece(): whole = lax.all_gather(both, axis, axis=dim, tiled=True)  13.6 us
    dot_general x1, matrix products, contract(): jnp.einsum('qmk,qkn->mn', left_filled, right_filled, preferred_element_ty...  13.3 us
    unnamed x2, starting transfers between devices  7.32 us
  transfers between devices with their start and end apart: 2, of which 1 were waited for; matrix products, arithmetic and copies ran while one was open for 0% of the time, Pallas kernels for 0%

commit v1 on v0

v1 whole, which is shorter than its diff:
```python
import jax
import jax.numpy as jnp
from jax import lax
from jax.experimental import pallas as pl
from jax.experimental.pallas import tpu as pltpu
from jax.sharding import PartitionSpec as P

MESH = pl.DeviceIdType.MESH
BF = jnp.bfloat16
F32 = jnp.float32
I32 = jnp.int32
SQ = 529


def iota(shape, dim):
    return lax.broadcasted_iota(I32, shape, dim)


def onehot(cond):
    return jnp.where(cond, 1.0, 0.0).astype(BF)


def div25(lane):
    return (lane * 41) >> 10


def div23(n):
    return (n * 2850) >> 16


def prepare(left_ref, right_ref, lw_ref, rw_ref):
    lane = iota((1, 128), 1)
    field = iota((SQ + 1, 128), 0)
    left = left_ref[...]
    tiles = []
    for t in range(5):
        target = jnp.where(lane < 115, 115 * t + lane, 9999)
        target = jnp.where(target < SQ, target, 9999)
        target = jnp.where(lane == 120, SQ, target)
        tiles.append(jnp.dot(left, onehot(field == target), preferred_element_type=F32))
    for d in range(8):
        rows = [tile[24 * d : 24 * d + 24] for tile in tiles] + [jnp.zeros((8, 128), F32)]
        lw_ref[d] = jnp.concatenate(rows, axis=0).astype(BF)
    right = right_ref[...]
    row = iota((288, 1), 0)
    group = (row * 2731) >> 16
    c = row - 24 * group
    f = iota((288, SQ + 1), 1)
    f_c = f - 23 * div23(f)
    keep = jnp.where(f == SQ, 23, f_c) == c
    q_of = div25(lane)
    b_of = lane - 25 * q_of
    total = jnp.zeros((288, 128), F32)
    for q in range(5):
        pick = onehot(iota((288, 60), 1) == group + 12 * q)
        spread = jnp.dot(pick, right, preferred_element_type=F32)
        spread = jnp.where(keep, spread, 0.0).astype(BF)
        low = jnp.where(q_of == q, 23 * b_of, 9999)
        hit = jnp.where((field >= low) & (field < low + 23) & (field < SQ), 1.0, 0.0)
        code = jnp.where((field == SQ) & (q_of == q), 1.0, 0.0)
        total += jnp.dot(spread, (hit + code).astype(BF), preferred_element_type=F32)
    for t in range(4):
        rw_ref[t] = total[72 * t : 72 * t + 72].astype(BF)


def multiply(
    lws, rws, out, LW, RW, PX, VE, LD, RT, ACC, OS,
    a_s, a_r, b_s, b_r, z_s, z_r, x_s, x_r, xh_s, xh_r, y_s, y_r, yh_s, yh_r, d_s, d_r, o_s, o_r, l_sem,
):
    r, y, z = lax.axis_index("row"), lax.axis_index("col"), lax.axis_index("depth")
    x, e = r // 2, r % 2
    mod = lax.rem

    def zat(o):
        return (r, y, mod(z + o + 8, 8))

    def yat(o):
        return (r, mod(y + o + 4, 4), z)

    def xat(o):
        return (mod(r + 2 * o + 8, 8), y, z)

    partner = (r + 1 - 2 * e, y, z)
    friends = [zat(o) for o in range(1, 8)] + [yat(o) for o in range(1, 4)] + [xat(1), xat(-1), partner]
    barrier = pltpu.get_barrier_semaphore()
    for who in friends:
        pl.semaphore_signal(barrier, inc=1, device_id=who, device_id_type=MESH)
    pl.semaphore_wait(barrier, len(friends))

    def copy(src, dst, send, recv, who):
        return pltpu.make_async_remote_copy(
            src_ref=src, dst_ref=dst, send_sem=send, recv_sem=recv, device_id=who, device_id_type=MESH
        )

    def unit(k):
        odd = k % 2
        return mod(z + (1 - 2 * odd) * ((k + 1) // 2) + 8, 8)

    def a_copy(o):
        to = mod(y + o, 4)
        return copy(rws.at[to], RW.at[z, e, x, y], a_s.at[o - 1], a_r.at[o - 1], (r, to, z))

    def b_copy(k):
        odd = k % 2
        to = mod(z - (1 - 2 * odd) * ((k + 1) // 2) + 8, 8)
        return copy(lws.at[to], LW.at[y, z], b_s.at[k], b_r.at[k], (r, y, to))

    def z_copy(k):
        odd = k % 2
        step = 2 * odd - 1
        u = mod(z - (2 * odd - 1) * ((k + 1) // 2 - 1) + 8, 8)
        ref = RW.at[u, e, x]
        return copy(ref, ref, z_s.at[k], z_r.at[k], (r, y, mod(z + step + 8, 8)))

    def zh_copy(h):
        u = unit(5 + h)
        ref = RW.at[u, e, x, pl.ds(2 * h, 2)]
        return copy(ref, ref, z_s.at[7 + h], z_r.at[7 + h], zat(1 - 2 * h))

    def x_copy(k, h):
        ref = RW.at[unit(k), e, x]
        return copy(ref, ref, x_s.at[h, k], x_r.at[h, k], xat(1 - 2 * h))

    def xh_copy(k, h):
        ref = RW.at[unit(k), e, mod(x - (1 - 2 * h) + 4, 4), pl.ds(2 * h, 2)]
        return copy(ref, ref, xh_s.at[h, k], xh_r.at[h, k], xat(1 - 2 * h))

    def y_copy(k, h):
        ref = LW.at[y, unit(k)]
        return copy(ref, ref, y_s.at[h, k], y_r.at[h, k], yat(1 - 2 * h))

    def yh_copy(k, h):
        ref = LW.at[mod(y - (1 - 2 * h) + 4, 4), unit(k), pl.ds(64 * h, 64)]
        return copy(ref, ref, yh_s.at[h, k], yh_r.at[h, k], yat(1 - 2 * h))

    def d_copy(k):
        ref = RW.at[unit(k), e]
        return copy(ref, ref, d_s.at[k], d_r.at[k], partner)

    for o in range(1, 4):
        a_copy(o).start()
    for k in range(1, 8):
        b_copy(k).start()
    own_right = pltpu.make_async_copy(rws.at[y], RW.at[z, e, x, y], l_sem.at[0])
    own_right.start()
    own_left = pltpu.make_async_copy(lws.at[z], LW.at[y, z], l_sem.at[1])
    own_left.start()

    lane = iota((1, 128), 1)
    q_of = div25(lane)
    b_of = lane - 25 * q_of
    pr = iota((160, 1), 0)
    pt, ps, pi = pr >> 5, (pr >> 3) & 3, pr & 7
    perm = onehot(jnp.where(pi < 6, 24 * pt + 4 * pi + ps, 9999) == iota((160, 128), 1))
    el = iota((128, 1), 0)
    expand = []
    for a in range(5):
        expand.append(onehot(jnp.where((b_of < 23) & (q_of < 5), 23 * a + b_of, 9999) == el))
    expand.append(onehot(jnp.broadcast_to(el == 120, (128, 128))))
    expand = jnp.concatenate(expand, axis=1)
    q_f = q_of.astype(F32)
    j_id = iota((32, 128), 0).astype(F32).astype(BF)

    ACC[...] = jnp.zeros_like(ACC)

    def consume(u):
        for p in range(4):
            px = jnp.dot(perm, LW[p, u], preferred_element_type=F32).astype(BF)
            for t in range(5):
                PX[t, pl.ds(32 * p, 32), :] = px[32 * t : 32 * t + 32]
        for t in range(5):
            width = 768 if t == 0 else 640
            ve = jnp.dot(PX[t], expand[:, :width], preferred_element_type=F32)
            for a in range(5):
                if 5 * t + a < 24:
                    VE[5 * t + a] = ve[:, 128 * a : 128 * a + 128]
            if t == 0:
                VE[24] = ve[:, 640:768] - q_f

        def left_tile(i, carry):
            p, m = i // 8, i % 8
            base = pl.multiple_of(p * 32, 32)
            col = pl.multiple_of(i * 128, 128)
            want = (5 * m).astype(F32)
            masks = [VE[24, pl.ds(base + 8 * s, 8), :] == want for s in range(4)]
            for ap in range(12):
                pair = []
                for a in (2 * ap, 2 * ap + 1):
                    v = jnp.zeros((8, 128), F32)
                    for s in range(4):
                        v = jnp.where(masks[s], VE[a, pl.ds(base + 8 * s, 8), :], v)
                    pair.append(v)
                LD[pl.ds(16 * ap, 16), pl.ds(col, 128)] = jnp.concatenate(pair, axis=0).astype(BF)
            return carry

        lax.fori_loop(0, 32, left_tile, 0)

        def right_tile(i, carry):
            p, m = i // 8, i % 8
            col = pl.multiple_of(i * 128, 128)
            block = RW[u, m % 2, m // 2, p]
            masks = [jnp.broadcast_to(block[24 * s + 23 : 24 * s + 24], (32, 128)) == j_id for s in range(3)]
            for c in range(23):
                v = jnp.zeros((32, 128), BF)
                for s in range(3):
                    v = jnp.where(masks[s], jnp.broadcast_to(block[24 * s + c : 24 * s + c + 1], (32, 128)), v)
                RT[pl.ds(32 * c, 32), pl.ds(col, 128)] = v
            return carry

        lax.fori_loop(0, 32, right_tile, 0)
        ACC[...] += lax.dot_general(RT[...], LD[...], (((1,), (1,)), ((), ())), preferred_element_type=F32)

    for o in range(1, 4):
        a_copy(o).wait_recv()
    own_right.wait()
    own_left.wait()
    z_copy(1).start()
    z_copy(2).start()

    def step(k, carry):
        @pl.when((k >= 1) & (k <= 6))
        def _():
            z_copy(k).wait_recv()

        @pl.when((k >= 1) & (k <= 4))
        def _():
            z_copy(k + 2).start()

        @pl.when((k == 5) | (k == 6))
        def _():
            zh_copy(k - 5).start()

        @pl.when(k == 7)
        def _():
            zh_copy(0).wait_recv()
            zh_copy(1).wait_recv()

        @pl.when(k <= 7)
        def _():
            x_copy(k, 0).start()
            x_copy(k, 1).start()

            @pl.when(k >= 1)
            def _():
                b_copy(k).wait_recv()

            y_copy(k, 0).start()
            y_copy(k, 1).start()

        @pl.when((k >= 1) & (k <= 8))
        def _():
            for h in range(2):
                x_copy(k - 1, h).wait_recv()
                xh_copy(k - 1, h).start()
            for h in range(2):
                y_copy(k - 1, h).wait_recv()
                yh_copy(k - 1, h).start()

        @pl.when((k >= 2) & (k <= 9))
        def _():
            for h in range(2):
                xh_copy(k - 2, h).wait_recv()
            d_copy(k - 2).start()
            for h in range(2):
                yh_copy(k - 2, h).wait_recv()

        @pl.when(k >= 3)
        def _():
            d_copy(k - 3).wait_recv()
            consume(unit(k - 3))

        return carry

    lax.fori_loop(0, 11, step, 0)

    mr = iota((144, 1), 0)
    mi = div23(mr)
    ma = mr - 23 * mi
    rows_pick = onehot(jnp.where(mr < 138, 8 * ma + mi, 9999) == iota((144, 192), 1))
    res = ACC[...].astype(BF)
    turned = lax.dot_general(rows_pick, res, (((1,), (1,)), ((), ())), preferred_element_type=F32).astype(BF)
    jj = div23(lane)
    cc = lane - 23 * jj
    ni = iota((736, 1), 0)
    for d in range(8):
        target = jnp.where(lane < 92, 32 * cc + 4 * d + jj, 9999)
        OS[d] = jnp.dot(turned, onehot(ni == target), preferred_element_type=F32).astype(BF)

    def o_copy(o):
        to = mod(z + o, 8)
        return copy(OS.at[to], out.at[z], o_s.at[o], o_r.at[o], (r, y, to))

    for o in range(1, 8):
        o_copy(o).start()
    own_out = pltpu.make_async_copy(OS.at[z], out.at[z], l_sem.at[2])
    own_out.start()

    for o in range(1, 4):
        a_copy(o).wait_send()

    def sent(k, carry):
        @pl.when(k >= 1)
        def _():
            b_copy(k).wait_send()

        @pl.when((k >= 1) & (k <= 6))
        def _():
            z_copy(k).wait_send()

        for h in range(2):
            x_copy(k, h).wait_send()
            xh_copy(k, h).wait_send()
            y_copy(k, h).wait_send()
            yh_copy(k, h).wait_send()
        d_copy(k).wait_send()
        return carry

    lax.fori_loop(0, 8, sent, 0)
    zh_copy(0).wait_send()
    zh_copy(1).wait_send()
    own_out.wait()
    for o in range(1, 8):
        o_copy(o).wait()


def body(left_values, left_columns, right_values, right_columns):
    left = jnp.concatenate([left_values, left_columns[..., None].astype(BF)], axis=3).reshape(192, SQ + 1)
    right = jnp.concatenate([right_values, right_columns[..., None].astype(BF)], axis=4).reshape(60, SQ + 1)
    vmem = pl.BlockSpec(memory_space=pltpu.VMEM)
    lws, rws = pl.pallas_call(
        prepare,
        out_shape=(jax.ShapeDtypeStruct((8, 128, 128), BF), jax.ShapeDtypeStruct((4, 72, 128), BF)),
        in_specs=[vmem, vmem],
        out_specs=(vmem, vmem),
        name="prepare",
    )(left, right)
    dma = pltpu.SemaphoreType.DMA
    pieces = pl.pallas_call(
        multiply,
        out_shape=jax.ShapeDtypeStruct((8, 144, 128), BF),
        in_specs=[vmem, vmem],
        out_specs=vmem,
        scratch_shapes=[
            pltpu.VMEM((4, 8, 128, 128), BF),
            pltpu.VMEM((8, 2, 4, 4, 72, 128), BF),
            pltpu.VMEM((5, 128, 128), BF),
            pltpu.VMEM((25, 128, 128), F32),
            pltpu.VMEM((192, 4096), BF),
            pltpu.VMEM((736, 4096), BF),
            pltpu.VMEM((736, 192), F32),
            pltpu.VMEM((8, 144, 128), BF),
            dma((3,)), dma((3,)),
            dma((8,)), dma((8,)),
            dma((9,)), dma((9,)),
            dma((2, 8)), dma((2, 8)),
            dma((2, 8)), dma((2, 8)),
            dma((2, 8)), dma((2, 8)),
            dma((2, 8)), dma((2, 8)),
            dma((8,)), dma((8,)),
            dma((8,)), dma((8,)),
            dma((3,)),
        ],
        compiler_params=pltpu.CompilerParams(collective_id=0, has_side_effects=True, vmem_limit_bytes=60 << 20),
        name="multiply",
    )(lws, rws)
    return pieces[:, :138, :92].reshape(1104, 92)


def solution(mesh):
    placed = (
        P("row", ("col", "depth"), None, None),
        P("row", ("col", "depth"), None),
        P(("col", "depth"), "row", None, None, None),
        P(("col", "depth"), "row", None, None),
    )
    return jax.shard_map(
        body, mesh=mesh, in_specs=placed, out_specs=P("row", ("col", "depth")), check_vma=False
    )
```

time: 359 us -> 92.8 us (0.26)
  the two profiles are of different devices: /device:TPU:56 before, /device:TPU:16 now
where the time goes in v1:
time: 92.8 us; the launch traced here: 92.6 us
  Pallas kernels  87 us (94%)
  other arithmetic  2.9 us (3%)
  local copies, waits for them, and re-layouts  2.67 us (3%)
    pallas_call x1, Pallas kernels, body(): pl.pallas_call(multiply, out_shape=jax.ShapeDtypeStruct((8, 144, 128), BF...  83.6 us
    pallas_call x1, Pallas kernels, body(): pl.pallas_call(prepare, out_shape=(jax.ShapeDtypeStruct((8, 128, 128), BF...  3.34 us
    reshape x2, local copies, waits for them, and re-layouts, body(): return pieces[:, :138, :92].reshape(1104, 92)  1.93 us

profile of v1, /device:TPU:16, one launch (start us, length us, event | category | flops | bytes accessed | tf_op | source)
XLA Modules:
  0.0 92.6 jit_solution(8778160528332741427)
XLA Ops:
  0.0 0.0 copy-start.1
  0.0 0.7 convert_element_type.30
  0.7 0.7 convert_element_type.32
  1.4 0.1 copy.13
  1.5 0.1 convert_element_type.35
  1.6 0.1 copy.10
  1.7 0.1 convert_element_type.34
  1.8 0.0 copy-done.1
  1.9 0.0 copy-start
  1.9 0.1 concatenate.14
  2.0 0.7 pad_maximum_fusion.1.right_ref
  2.7 0.1 copy-done
  2.8 0.1 concatenate.12
  2.9 0.8 pad_maximum_fusion.left_ref
  3.7 3.3 %prepare.1 = (bf16[8,128,128]{2,1,0:T(8,128)(2,1)}, bf16[4,72,128]{2,1,0:T(8,128)(2,1)}) custom-call(bf16[192,530]{1,0:T(8,128)(2,1)} %pad_maximum_fusion.left_ref, bf16[60,530]{1,0:T(8,128)(2,1)} %pad_maximum_fusion.1.right_ref), custom_call_target="tpu_custom_call" | custom-call | tf_op jit(solution)/shard_map/prepare/pallas_call | solution.py:330
  7.0 83.6 %multiply.1 = bf16[8,144,128]{2,1,0:T(8,128)(2,1)} custom-call(bf16[8,128,128]{2,1,0:T(8,128)(2,1)} %get-tuple-element.7.lws, bf16[4,72,128]{2,1,0:T(8,128)(2,1)} %get-tuple-element.8.rws), custom_call_target="tpu_custom_call" | custom-call | tf_op jit(solution)/shard_map/multiply/pallas_call | solution.py:338
  90.7 1.0 %reshape.37 = bf16[1104,92]{1,0:T(8,128)(2,1)S(1)} reshape(bf16[8,138,92]{2,1,0:T(8,128)(2,1)} %bitcast.3) | data formatting | bytes 406272 | tf_op jit(solution)/shard_map/reshape | solution.py:366
  91.7 0.9 copy.15
  (1 shorter events, 0.0 us)
Async XLA Ops:
  0.0 1.8 %copy-start.1 = (bf16[1,5,4,3,529]{4,2,3,1,0:T(4,128)(2,1)S(1)}, bf16[1,5,4,3,529]{4,2,3,1,0:T(4,128)(2,1)}, u32[]{:S(2)}) copy-start(bf16[1,5,4,3,529]{4,2,3,1,0:T(4,128)(2,1)} %param.6) | copy-start | bytes 190444
  1.9 0.9 %copy-start = (bf16[48,1,4,529]{3,2,1,0:T(4,128)(2,1)S(1)}, bf16[48,1,4,529]{3,2,1,0:T(4,128)(2,1)}, u32[]{:S(2)}) copy-start(bf16[48,1,4,529]{3,2,1,0:T(4,128)(2,1)} %param.4) | copy-start | bytes 609412

commit v2 on v1

v2 whole, which is shorter than its diff:
```python
import jax
import jax.numpy as jnp
from jax import lax
from jax.experimental import pallas as pl
from jax.experimental.pallas import tpu as pltpu
from jax.sharding import PartitionSpec as P

MESH = pl.DeviceIdType.MESH
BF = jnp.bfloat16
F32 = jnp.float32
I32 = jnp.int32
SQ = 529


def iota(shape, dim):
    return lax.broadcasted_iota(I32, shape, dim)


def onehot(cond):
    return jnp.where(cond, 1.0, 0.0).astype(BF)


def div25(lane):
    return (lane * 41) >> 10


def div23(n):
    return (n * 2850) >> 16


def fill_right(right, codes, rws):
    lane = iota((1, 128), 1)
    field = iota((SQ, 128), 0)
    row = iota((288, 1), 0)
    group = (row * 2731) >> 16
    c = row - 24 * group
    t = (group * 11) >> 5
    u = group - 3 * t
    f = iota((288, SQ), 1)
    keep = f - 23 * div23(f) == c
    q_of = div25(lane)
    b_of = lane - 25 * q_of
    total = jnp.zeros((288, 128), F32)
    for q in range(5):
        pick = onehot(iota((288, 60), 1) == 12 * q + 4 * u + t)
        spread = jnp.dot(pick, right, preferred_element_type=F32)
        spread = jnp.where(keep, spread, 0.0).astype(BF)
        low = jnp.where(q_of == q, 23 * b_of, 9999)
        total += jnp.dot(spread, onehot((field >= low) & (field < low + 23)), preferred_element_type=F32)
    q_hot = onehot(iota((5, 128), 0) == q_of)
    for v in range(3):
        wide = jnp.dot(codes[v].astype(F32).astype(BF), q_hot, preferred_element_type=F32).astype(BF)
        pick = onehot(iota((288, 4), 1) == jnp.where((u == v) & (c == 23), t, 9999))
        total += jnp.dot(pick, wide, preferred_element_type=F32)
    for k in range(4):
        rws[k] = total[72 * k : 72 * k + 72].astype(BF)


def fill_left(left, codes, lws):
    lane = iota((1, 128), 1)
    field = iota((SQ, 128), 0)
    row = iota((192, 1), 0)
    pick = onehot(iota((192, 48), 1) == row >> 2)
    codes = codes.astype(F32).astype(BF)
    code = lax.dot_general(pick, codes, (((1,), (1,)), ((), ())), preferred_element_type=F32)
    code = jnp.where(iota((192, 4), 1) == (row & 3), code, 0.0).astype(BF)
    tiles = []
    for t in range(5):
        target = jnp.where(lane < 115, 115 * t + lane, 9999)
        tile = jnp.dot(left, onehot(field == target), preferred_element_type=F32)
        if t == 0:
            place = onehot(jnp.broadcast_to(lane == 120, (4, 128)))
            tile += jnp.dot(code, place, preferred_element_type=F32)
        tiles.append(tile)
    for d in range(8):
        rows = [tile[24 * d : 24 * d + 24] for tile in tiles] + [jnp.zeros((8, 128), F32)]
        lws[d] = jnp.concatenate(rows, axis=0).astype(BF)


def multiply(
    left_ref, lcol_ref, right_ref, rcol_ref, out, lws, rws, LW, RW, LDA, LDB, ACC, OTHER, GS, OS,
    a_s, a_r, b_s, b_r, z_s, z_r, x_s, x_r, xh_s, xh_r, y_s, y_r, yh_s, yh_r, d_s, d_r, o_s, o_r, p_sem, l_sem,
):
    r, y, z = lax.axis_index("row"), lax.axis_index("col"), lax.axis_index("depth")
    x, e = r // 2, r % 2
    mod = lax.rem

    def zat(o):
        return (r, y, mod(z + o + 8, 8))

    def yat(o):
        return (r, mod(y + o + 4, 4), z)

    def xat(o):
        return (mod(r + 2 * o + 8, 8), y, z)

    partner = (r + 1 - 2 * e, y, z)
    friends = [zat(o) for o in range(1, 8)] + [yat(o) for o in range(1, 4)] + [xat(1), xat(-1), partner]
    barrier = pltpu.get_barrier_semaphore()
    for who in friends:
        pl.semaphore_signal(barrier, inc=1, device_id=who, device_id_type=MESH)
    fill_right(right_ref[...], rcol_ref, rws)

    def copy(src, dst, send, recv, who):
        return pltpu.make_async_remote_copy(
            src_ref=src, dst_ref=dst, send_sem=send, recv_sem=recv, device_id=who, device_id_type=MESH
        )

    def unit(k):
        odd = k % 2
        return mod(z + (1 - 2 * odd) * ((k + 1) // 2) + 8, 8)

    def a_copy(o):
        to = mod(y + o, 4)
        return copy(rws.at[to], RW.at[z, x, y], a_s.at[o - 1], a_r.at[o - 1], (r, to, z))

    def b_copy(k):
        odd = k % 2
        to = mod(z - (1 - 2 * odd) * ((k + 1) // 2) + 8, 8)
        return copy(lws.at[to], LW.at[e, y, z], b_s.at[k], b_r.at[k], (r, y, to))

    def z_copy(k):
        odd = k % 2
        step = 2 * odd - 1
        u = mod(z - (2 * odd - 1) * ((k + 1) // 2 - 1) + 8, 8)
        ref = RW.at[u, x]
        return copy(ref, ref, z_s.at[k], z_r.at[k], (r, y, mod(z + step + 8, 8)))

    def zh_copy(h):
        u = unit(5 + h)
        ref = RW.at[u, x, pl.ds(2 * h, 2)]
        return copy(ref, ref, z_s.at[7 + h], z_r.at[7 + h], zat(1 - 2 * h))

    def x_copy(k, h):
        ref = RW.at[unit(k), x]
        return copy(ref, ref, x_s.at[h, k], x_r.at[h, k], xat(1 - 2 * h))

    def xh_copy(k, h):
        ref = RW.at[unit(k), mod(x - (1 - 2 * h) + 4, 4), pl.ds(2 * h, 2)]
        return copy(ref, ref, xh_s.at[h, k], xh_r.at[h, k], xat(1 - 2 * h))

    def y_copy(k, h):
        ref = LW.at[e, y, unit(k)]
        return copy(ref, ref, y_s.at[h, k], y_r.at[h, k], yat(1 - 2 * h))

    def yh_copy(k, h):
        ref = LW.at[e, mod(y - (1 - 2 * h) + 4, 4), unit(k), pl.ds(64 * h, 64)]
        return copy(ref, ref, yh_s.at[h, k], yh_r.at[h, k], yat(1 - 2 * h))

    def d_copy(k):
        ref = LW.at[e, pl.ds(0, 4), unit(k)]
        return copy(ref, ref, d_s.at[k], d_r.at[k], partner)

    fill_left(left_ref[...], lcol_ref[...], lws)
    lane = iota((1, 128), 1)
    q_of = div25(lane)
    b_of = lane - 25 * q_of
    pr = iota((160, 1), 0)
    pt, ps, pi = pr >> 5, (pr >> 3) & 3, pr & 7
    perm = onehot(jnp.where(pi < 6, 24 * pt + 4 * pi + ps, 9999) == iota((160, 128), 1))
    el = iota((128, 1), 0)
    expand = []
    for a in range(5):
        expand.append(onehot(jnp.where((b_of < 23) & (q_of < 5), 23 * a + b_of, 9999) == el))
    expand.append(onehot(jnp.broadcast_to(el == 120, (128, 128))))
    expand = jnp.concatenate(expand, axis=1)
    q_f = (q_of + 5 * e).astype(F32)
    j_id = iota((32, 128), 0).astype(F32).astype(BF)

    ACC[...] = jnp.zeros_like(ACC)
    jj = div23(lane)
    cc = lane - 23 * jj
    ni = iota((736, 1), 0)
    for d in range(8):
        target = jnp.where(lane < 92, 32 * cc + 4 * d + jj, 9999)
        GS[:, pl.ds(128 * d, 128)] = onehot(ni == target)

    pl.semaphore_wait(barrier, len(friends))
    for o in range(1, 4):
        a_copy(o).start()
    own_right = pltpu.make_async_copy(rws.at[y], RW.at[z, x, y], l_sem.at[0])
    own_right.start()
    for k in range(1, 8):
        b_copy(k).start()
    own_left = pltpu.make_async_copy(lws.at[z], LW.at[e, y, z], l_sem.at[1])
    own_left.start()


    def fill(u, j, ld):
        px = []
        for st in range(2):
            for i in range(2):
                px.append(jnp.dot(perm, LW[st, 2 * j + i, u], preferred_element_type=F32).astype(BF))
        every = jnp.dot(jnp.concatenate(px, axis=0), expand, preferred_element_type=F32)
        for st in range(2):
            for i in range(2):
                ve = every[160 * (2 * st + i) : 160 * (2 * st + i) + 160]
                masks = []
                for s in range(4):
                    code = ve[8 * s : 8 * s + 8, 640:768] - q_f
                    code = jnp.concatenate([code, code], axis=0).astype(BF)
                    masks.append([code == jnp.array(10 * m, BF) for m in range(4)])
                for ap in range(12):
                    slots = []
                    for s in range(4):
                        pair = []
                        for a in (2 * ap, 2 * ap + 1):
                            t, w = a // 5, a % 5
                            pair.append(ve[32 * t + 8 * s : 32 * t + 8 * s + 8, 128 * w : 128 * w + 128])
                        slots.append(jnp.concatenate(pair, axis=0).astype(BF))
                    for m in range(4):
                        v = jnp.zeros((16, 128), BF)
                        for s in range(4):
                            v = jnp.where(masks[s][m], slots[s], v)
                        ld[st, pl.ds(16 * ap, 16), pl.ds(512 * i + 128 * m, 128)] = v

    def take(u, j, ld):
        tiles = []
        for m in range(8):
            block = RW[u, m % 4, 2 * j + m // 4]
            masks = [jnp.broadcast_to(block[24 * s + 23 : 24 * s + 24], (32, 128)) == j_id for s in range(3)]
            rows = []
            for c in range(23):
                v = jnp.zeros((32, 128), BF)
                for s in range(3):
                    v = jnp.where(masks[s], jnp.broadcast_to(block[24 * s + c : 24 * s + c + 1], (32, 128)), v)
                rows.append(v)
            tiles.append(jnp.concatenate(rows, axis=0))
        full = jnp.concatenate(tiles, axis=1)
        for st in range(2):
            ACC[st] += lax.dot_general(full, ld[st], (((1,), (1,)), ((), ())), preferred_element_type=F32)

    def x_start(k):
        x_copy(k, 0).start()
        x_copy(k, 1).start()

    def y_start(k):
        y_copy(k, 0).start()
        y_copy(k, 1).start()

    def x_forward(k):
        for h in range(2):
            x_copy(k, h).wait_recv()
            xh_copy(k, h).start()

    def y_forward(k):
        for h in range(2):
            y_copy(k, h).wait_recv()
            yh_copy(k, h).start()

    def x_done(k):
        for h in range(2):
            xh_copy(k, h).wait_recv()

    def y_done(k):
        for h in range(2):
            yh_copy(k, h).wait_recv()

    own_left.wait()
    y_start(0)
    for k in (1, 2):
        b_copy(k).wait_recv()
        y_start(k)
    for o in range(1, 4):
        a_copy(o).wait_recv()
    own_right.wait()
    z_copy(1).start()
    z_copy(2).start()
    x_start(0)
    y_forward(0)
    for k in (3, 4):
        b_copy(k).wait_recv()
        y_start(k)
    y_done(0)
    d_copy(0).start()
    for k in (1, 2):
        z_copy(k).wait_recv()
        z_copy(k + 2).start()
    x_start(1)
    x_forward(0)
    x_start(2)
    y_forward(1)
    y_forward(2)
    for k in (5, 6, 7):
        b_copy(k).wait_recv()
        y_start(k)
    d_copy(0).wait_recv()
    fill(unit(0), 0, LDA)
    x_forward(1)
    y_forward(3)
    y_forward(4)
    for k in (3, 4):
        z_copy(k).wait_recv()
        z_copy(k + 2).start()
    x_start(3)

    def step(k, carry):
        u = unit(k)

        @pl.when(k == 1)
        def _():
            for v in (5, 6):
                z_copy(v).wait_recv()
                zh_copy(v - 5).start()

        @pl.when(k <= 6)
        def _():
            y_done(k + 1)
            d_copy(k + 1).start()

        x_done(k)
        fill(u, 1, LDB)
        take(u, 0, LDA)

        @pl.when(k == 3)
        def _():
            zh_copy(0).wait_recv()
            zh_copy(1).wait_recv()

        @pl.when(k <= 5)
        def _():
            x_forward(k + 2)

        @pl.when(k <= 3)
        def _():
            x_start(k + 4)

        @pl.when(k == 0)
        def _():
            for v in (5, 6, 7):
                y_forward(v)

        @pl.when(k <= 6)
        def _():
            d_copy(k + 1).wait_recv()

        fill(unit(jnp.minimum(k + 1, 7)), 0, LDA)
        take(u, 1, LDB)
        return carry

    lax.fori_loop(0, 8, step, 0)
    p_copy = copy(ACC.at[1 - e], OTHER, p_sem.at[0], p_sem.at[1], partner)
    p_copy.start()
    p_copy.wait_recv()

    mr = iota((144, 1), 0)
    mi = div23(mr)
    ma = mr - 23 * mi
    rows_pick = onehot(jnp.where(mr < 138, 8 * ma + mi, 9999) == iota((144, 192), 1))
    res = (ACC[e] + OTHER[...]).astype(BF)
    turned = lax.dot_general(rows_pick, res, (((1,), (1,)), ((), ())), preferred_element_type=F32).astype(BF)
    spread = jnp.dot(turned, GS[...], preferred_element_type=F32).astype(BF)
    for d in range(8):
        OS[d] = spread[:, 128 * d : 128 * d + 128]

    def o_copy(o):
        to = mod(z + o, 8)
        return copy(OS.at[to], out.at[z], o_s.at[o], o_r.at[o], (r, y, to))

    for o in range(1, 8):
        o_copy(o).start()
    own_out = pltpu.make_async_copy(OS.at[z], out.at[z], l_sem.at[2])
    own_out.start()

    for o in range(1, 4):
        a_copy(o).wait_send()

    def sent(k, carry):
        @pl.when(k >= 1)
        def _():
            b_copy(k).wait_send()

        @pl.when((k >= 1) & (k <= 6))
        def _():
            z_copy(k).wait_send()

        for h in range(2):
            x_copy(k, h).wait_send()
            xh_copy(k, h).wait_send()
            y_copy(k, h).wait_send()
            yh_copy(k, h).wait_send()
        d_copy(k).wait_send()
        return carry

    lax.fori_loop(0, 8, sent, 0)
    zh_copy(0).wait_send()
    zh_copy(1).wait_send()
    own_out.wait()
    p_copy.wait_send()
    for o in range(1, 8):
        o_copy(o).wait()


def body(left_values, left_columns, right_values, right_columns):
    left = left_values.reshape(192, SQ)
    left_codes = jnp.transpose(left_columns[:, 0], (1, 0))
    right = jnp.transpose(right_values[0], (0, 2, 1, 3)).reshape(60, SQ)
    right_codes = jnp.transpose(right_columns[0], (2, 1, 0))
    vmem = pl.BlockSpec(memory_space=pltpu.VMEM)
    dma = pltpu.SemaphoreType.DMA
    pieces = pl.pallas_call(
        multiply,
        out_shape=jax.ShapeDtypeStruct((8, 144, 128), BF),
        in_specs=[vmem] * 4,
        out_specs=vmem,
        scratch_shapes=[
            pltpu.VMEM((8, 128, 128), BF),
            pltpu.VMEM((4, 72, 128), BF),
            pltpu.VMEM((2, 4, 8, 128, 128), BF),
            pltpu.VMEM((8, 4, 4, 72, 128), BF),
            pltpu.VMEM((2, 192, 1024), BF),
            pltpu.VMEM((2, 192, 1024), BF),
            pltpu.VMEM((2, 736, 192), F32),
            pltpu.VMEM((736, 192), F32),
            pltpu.VMEM((736, 1024), BF),
            pltpu.VMEM((8, 144, 128), BF),
            dma((3,)), dma((3,)),
            dma((8,)), dma((8,)),
            dma((9,)), dma((9,)),
            dma((2, 8)), dma((2, 8)),
            dma((2, 8)), dma((2, 8)),
            dma((2, 8)), dma((2, 8)),
            dma((2, 8)), dma((2, 8)),
            dma((8,)), dma((8,)),
            dma((8,)), dma((8,)),
            dma((2,)),
            dma((3,)),
        ],
        compiler_params=pltpu.CompilerParams(collective_id=0, has_side_effects=True, vmem_limit_bytes=24 << 20),
        name="multiply",
    )(left, left_codes, right, right_codes)
    return pieces[:, :138, :92].reshape(1104, 92)


def solution(mesh):
    placed = (
        P("row", ("col", "depth"), None, None),
        P("row", ("col", "depth"), None),
        P(("col", "depth"), "row", None, None, None),
        P(("col", "depth"), "row", None, None),
    )
    return jax.shard_map(
        body, mesh=mesh, in_specs=placed, out_specs=P("row", ("col", "depth")), check_vma=False
    )
```

time: 92.8 us -> 66.4 us (0.72)
  the two profiles are of different devices: /device:TPU:16 before, /device:TPU:1 now
where the time goes in v2:
time: 66.4 us; the launch traced here: 66.3 us
  Pallas kernels  63.3 us (95%)
  local copies, waits for them, and re-layouts  2.98 us (4%)
    pallas_call x1, Pallas kernels, body(): pl.pallas_call(multiply, out_shape=jax.ShapeDtypeStruct((8, 144, 128), BF...  63.3 us

profile of v2, /device:TPU:1, one launch (start us, length us, event | category | flops | bytes accessed | tf_op | source)
XLA Modules:
  0.0 66.3 jit_solution(15651113500730073885)
XLA Ops:
  0.0 0.9 %reshape.10.right_ref = bf16[60,529]{1,0:T(8,128)(2,1)S(1)} reshape(bf16[5,3,4,529]{3,2,1,0:T(4,128)(2,1)} %bitcast.13) | data formatting | bytes 126960 | tf_op jit(solution)/shard_map/reshape | solution.py:397
  0.9 0.0 copy-start
  0.9 0.0 copy-start.1
  1.0 1.1 %reshape.9.left_ref = bf16[192,529]{1,0:T(8,128)(2,1)S(1)} reshape(bf16[48,1,4,529]{3,2,1,0:T(4,128)(2,1)} %param.4) | data formatting | bytes 406272 | tf_op jit(solution)/shard_map/reshape | solution.py:395
  2.0 0.0 copy-done
  2.0 0.0 copy-done.1
  2.1 63.3 %multiply.1 = bf16[8,144,128]{2,1,0:T(8,128)(2,1)S(1)} custom-call(bf16[192,529]{1,0:T(8,128)(2,1)S(1)} %reshape.9.left_ref, s32[4,48]{1,0:T(4,128)S(1)} %bitcast.12, bf16[60,529]{1,0:T(8,128)(2,1)S(1)} %reshape.10.right_ref, s32[3,4,5]{2,1,0:T(4,128)S(1)} %bitcast.11), custom_call_target="tpu_custom_call" | custom-call | tf_op jit(solution)/shard_map/multiply/pallas_call | solution.py:401
  65.3 0.1 reshape.11
  65.4 0.9 %copy.6 = bf16[1104,92]{0,1:T(8,128)(2,1)} copy(bf16[1104,92]{1,0:T(8,128)(2,1)S(1)} %reshape.11) | data formatting | bytes 406272 | tf_op jit(solution)/shard_map/reshape | solution.py:432
Async XLA Ops:
  0.9 1.1 %copy-start = (s32[1,5,4,3]{1,2,3,0:T(4,128)S(1)}, s32[1,5,4,3]{1,2,3,0:T(4,128)}, u32[]{:S(2)}) copy-start(s32[1,5,4,3]{1,2,3,0:T(4,128)} %param.7) | copy-start | bytes 724
  0.9 1.1 %copy-start.1 = (s32[48,1,4]{0,2,1:T(4,128)S(1)}, s32[48,1,4]{0,2,1:T(4,128)}, u32[]{:S(2)}) copy-start(s32[48,1,4]{0,2,1:T(4,128)} %param.5) | copy-start | bytes 2308

commit v3 on v2

--- a/solution.py
+++ b/solution.py
@@ -59,22 +59,23 @@
 def fill_left(left, codes, lws):
     lane = iota((1, 128), 1)
     field = iota((SQ, 128), 0)
-    row = iota((192, 1), 0)
-    pick = onehot(iota((192, 48), 1) == row >> 2)
+    row = iota((256, 1), 0)
+    s, i = (row >> 3) & 3, row & 7
+    block_row = jnp.where(i < 6, 6 * (row >> 5) + i, 9999)
+    picked = jnp.dot(onehot(iota((256, 192), 1) == 4 * block_row + s), left, preferred_element_type=F32).astype(BF)
+    pick = onehot(iota((256, 48), 1) == block_row)
     codes = codes.astype(F32).astype(BF)
     code = lax.dot_general(pick, codes, (((1,), (1,)), ((), ())), preferred_element_type=F32)
-    code = jnp.where(iota((192, 4), 1) == (row & 3), code, 0.0).astype(BF)
-    tiles = []
+    code = jnp.where(iota((256, 4), 1) == s, code, 0.0).astype(BF)
     for t in range(5):
         target = jnp.where(lane < 115, 115 * t + lane, 9999)
-        tile = jnp.dot(left, onehot(field == target), preferred_element_type=F32)
+        tile = jnp.dot(picked, onehot(field == target), preferred_element_type=F32)
         if t == 0:
             place = onehot(jnp.broadcast_to(lane == 120, (4, 128)))
             tile += jnp.dot(code, place, preferred_element_type=F32)
-        tiles.append(tile)
-    for d in range(8):
-        rows = [tile[24 * d : 24 * d + 24] for tile in tiles] + [jnp.zeros((8, 128), F32)]
-        lws[d] = jnp.concatenate(rows, axis=0).astype(BF)
+        tile = tile.astype(BF)
+        for d in range(8):
+            lws[d, pl.ds(32 * t, 32), :] = tile[32 * d : 32 * d + 32]
 
 
 def multiply(
@@ -143,8 +144,11 @@
         ref = LW.at[e, y, unit(k)]
         return copy(ref, ref, y_s.at[h, k], y_r.at[h, k], yat(1 - 2 * h))
 
+    def y_first(h):
+        return copy(lws.at[z], LW.at[e, y, z], y_s.at[h, 0], y_r.at[h, 0], yat(1 - 2 * h))
+
     def yh_copy(k, h):
-        ref = LW.at[e, mod(y - (1 - 2 * h) + 4, 4), unit(k), pl.ds(64 * h, 64)]
+        ref = LW.at[e, mod(y - (1 - 2 * h) + 4, 4), unit(k), pl.ds(80 * h, 80)]
         return copy(ref, ref, yh_s.at[h, k], yh_r.at[h, k], yat(1 - 2 * h))
 
     def d_copy(k):
@@ -155,9 +159,6 @@
     lane = iota((1, 128), 1)
     q_of = div25(lane)
     b_of = lane - 25 * q_of
-    pr = iota((160, 1), 0)
-    pt, ps, pi = pr >> 5, (pr >> 3) & 3, pr & 7
-    perm = onehot(jnp.where(pi < 6, 24 * pt + 4 * pi + ps, 9999) == iota((160, 128), 1))
     el = iota((128, 1), 0)
     expand = []
     for a in range(5):
@@ -180,17 +181,19 @@
         a_copy(o).start()
     own_right = pltpu.make_async_copy(rws.at[y], RW.at[z, x, y], l_sem.at[0])
     own_right.start()
+    own_left = pltpu.make_async_copy(lws.at[z], LW.at[e, y, z], l_sem.at[1])
+    own_left.start()
+    for h in range(2):
+        y_first(h).start()
     for k in range(1, 8):
         b_copy(k).start()
-    own_left = pltpu.make_async_copy(lws.at[z], LW.at[e, y, z], l_sem.at[1])
-    own_left.start()
 
 
     def fill(u, j, ld):
         px = []
         for st in range(2):
             for i in range(2):
-                px.append(jnp.dot(perm, LW[st, 2 * j + i, u], preferred_element_type=F32).astype(BF))
+                px.append(LW[st, 2 * j + i, u])
         every = jnp.dot(jnp.concatenate(px, axis=0), expand, preferred_element_type=F32)
         for st in range(2):
             for i in range(2):
@@ -256,11 +259,6 @@
         for h in range(2):
             yh_copy(k, h).wait_recv()
 
-    own_left.wait()
-    y_start(0)
-    for k in (1, 2):
-        b_copy(k).wait_recv()
-        y_start(k)
     for o in range(1, 4):
         a_copy(o).wait_recv()
     own_right.wait()
@@ -268,9 +266,10 @@
     z_copy(2).start()
     x_start(0)
     y_forward(0)
-    for k in (3, 4):
+    for k in (1, 2):
         b_copy(k).wait_recv()
         y_start(k)
+    own_left.wait()
     y_done(0)
     d_copy(0).start()
     for k in (1, 2):
@@ -279,23 +278,48 @@
     x_start(1)
     x_forward(0)
     x_start(2)
+    for k in (3, 4):
+        b_copy(k).wait_recv()
+        y_start(k)
+    d_copy(0).wait_recv()
+    fill(unit(0), 0, LDA)
     y_forward(1)
     y_forward(2)
     for k in (5, 6, 7):
         b_copy(k).wait_recv()
         y_start(k)
-    d_copy(0).wait_recv()
-    fill(unit(0), 0, LDA)
-    x_forward(1)
-    y_forward(3)
-    y_forward(4)
-    for k in (3, 4):
-        z_copy(k).wait_recv()
-        z_copy(k + 2).start()
-    x_start(3)
 
     def step(k, carry):
         u = unit(k)
+
+        @pl.when(k == 1)
+        def _():
+            x_forward(2)
+            x_start(4)
+            y_forward(5)
+            y_forward(6)
+            y_forward(7)
+
+        @pl.when((k >= 1) & (k <= 6))
+        def _():
+            y_done(k + 1)
+            d_copy(k + 1).start()
+
+        x_done(k)
+        fill(u, 1, LDB)
+        take(u, 0, LDA)
+
+        @pl.when(k == 0)
+        def _():
+            y_done(1)
+            d_copy(1).start()
+            x_forward(1)
+            for v in (3, 4):
+                z_copy(v).wait_recv()
+                z_copy(v + 2).start()
+            x_start(3)
+            y_forward(3)
+            y_forward(4)
 
         @pl.when(k == 1)
         def _():
@@ -303,32 +327,18 @@
                 z_copy(v).wait_recv()
                 zh_copy(v - 5).start()
 
-        @pl.when(k <= 6)
-        def _():
-            y_done(k + 1)
-            d_copy(k + 1).start()
-
-        x_done(k)
-        fill(u, 1, LDB)
-        take(u, 0, LDA)
-
         @pl.when(k == 3)
         def _():
             zh_copy(0).wait_recv()
             zh_copy(1).wait_recv()
 
-        @pl.when(k <= 5)
+        @pl.when((k >= 1) & (k <= 5))
         def _():
             x_forward(k + 2)
 
-        @pl.when(k <= 3)
+        @pl.when((k >= 1) & (k <= 3))
         def _():
             x_start(k + 4)
-
-        @pl.when(k == 0)
-        def _():
-            for v in (5, 6, 7):
-                y_forward(v)
 
         @pl.when(k <= 6)
         def _():
@@ -357,7 +367,7 @@
         to = mod(z + o, 8)
         return copy(OS.at[to], out.at[z], o_s.at[o], o_r.at[o], (r, y, to))
 
-    for o in range(1, 8):
+    for o in (4, 3, 5, 2, 6, 1, 7):
         o_copy(o).start()
     own_out = pltpu.make_async_copy(OS.at[z], out.at[z], l_sem.at[2])
     own_out.start()
@@ -404,9 +414,9 @@
         in_specs=[vmem] * 4,
         out_specs=vmem,
         scratch_shapes=[
-            pltpu.VMEM((8, 128, 128), BF),
+            pltpu.VMEM((8, 160, 128), BF),
             pltpu.VMEM((4, 72, 128), BF),
-            pltpu.VMEM((2, 4, 8, 128, 128), BF),
+            pltpu.VMEM((2, 4, 8, 160, 128), BF),
             pltpu.VMEM((8, 4, 4, 72, 128), BF),
             pltpu.VMEM((2, 192, 1024), BF),
             pltpu.VMEM((2, 192, 1024), BF),

time: 66.4 us -> 66.3 us (level)
  no operation moved by 1% of the time
where the time goes in v3:
time: 66.3 us; the launch traced here: 66.1 us
  Pallas kernels  63.1 us (95%)
  local copies, waits for them, and re-layouts  2.98 us (4%)
    pallas_call x1, Pallas kernels, body(): pl.pallas_call(multiply, out_shape=jax.ShapeDtypeStruct((8, 144, 128), BF...  63.1 us

profile of v3, /device:TPU:1, one launch (start us, length us, event | category | flops | bytes accessed | tf_op | source)
XLA Modules:
  0.0 66.1 jit_solution(11435052479671636899)
XLA Ops:
  0.0 0.9 %reshape.10.right_ref = bf16[60,529]{1,0:T(8,128)(2,1)S(1)} reshape(bf16[5,3,4,529]{3,2,1,0:T(4,128)(2,1)} %bitcast.13) | data formatting | bytes 126960 | tf_op jit(solution)/shard_map/reshape | solution.py:407
  0.9 0.0 copy-start
  0.9 0.0 copy-start.1
  1.0 1.1 %reshape.9.left_ref = bf16[192,529]{1,0:T(8,128)(2,1)S(1)} reshape(bf16[48,1,4,529]{3,2,1,0:T(4,128)(2,1)} %param.4) | data formatting | bytes 406272 | tf_op jit(solution)/shard_map/reshape | solution.py:405
  2.0 0.0 copy-done
  2.0 0.0 copy-done.1
  2.1 63.1 %multiply.1 = bf16[8,144,128]{2,1,0:T(8,128)(2,1)S(1)} custom-call(bf16[192,529]{1,0:T(8,128)(2,1)S(1)} %reshape.9.left_ref, s32[4,48]{1,0:T(4,128)S(1)} %bitcast.12, bf16[60,529]{1,0:T(8,128)(2,1)S(1)} %reshape.10.right_ref, s32[3,4,5]{2,1,0:T(4,128)S(1)} %bitcast.11), custom_call_target="tpu_custom_call" | custom-call | tf_op jit(solution)/shard_map/multiply/pallas_call | solution.py:411
  65.1 0.1 reshape.11
  65.2 0.9 %copy.6 = bf16[1104,92]{0,1:T(8,128)(2,1)} copy(bf16[1104,92]{1,0:T(8,128)(2,1)S(1)} %reshape.11) | data formatting | bytes 406272 | tf_op jit(solution)/shard_map/reshape | solution.py:442
Async XLA Ops:
  0.9 1.1 %copy-start = (s32[1,5,4,3]{1,2,3,0:T(4,128)S(1)}, s32[1,5,4,3]{1,2,3,0:T(4,128)}, u32[]{:S(2)}) copy-start(s32[1,5,4,3]{1,2,3,0:T(4,128)} %param.7) | copy-start | bytes 724
  0.9 1.1 %copy-start.1 = (s32[48,1,4]{0,2,1:T(4,128)S(1)}, s32[48,1,4]{0,2,1:T(4,128)}, u32[]{:S(2)}) copy-start(s32[48,1,4]{0,2,1:T(4,128)} %param.5) | copy-start | bytes 2308

commit v4 on v3

--- a/solution.py
+++ b/solution.py
@@ -185,7 +185,7 @@
     own_left.start()
     for h in range(2):
         y_first(h).start()
-    for k in range(1, 8):
+    for k in (1, 2):
         b_copy(k).start()
 
 
@@ -266,26 +266,26 @@
     z_copy(2).start()
     x_start(0)
     y_forward(0)
+    for k in range(3, 8):
+        b_copy(k).start()
     for k in (1, 2):
         b_copy(k).wait_recv()
         y_start(k)
     own_left.wait()
     y_done(0)
     d_copy(0).start()
-    for k in (1, 2):
-        z_copy(k).wait_recv()
-        z_copy(k + 2).start()
+    x_forward(0)
+    z_copy(1).wait_recv()
+    z_copy(3).start()
     x_start(1)
-    x_forward(0)
+    z_copy(2).wait_recv()
+    z_copy(4).start()
     x_start(2)
-    for k in (3, 4):
-        b_copy(k).wait_recv()
-        y_start(k)
     d_copy(0).wait_recv()
     fill(unit(0), 0, LDA)
     y_forward(1)
     y_forward(2)
-    for k in (5, 6, 7):
+    for k in (3, 4):
         b_copy(k).wait_recv()
         y_start(k)
 
@@ -311,9 +311,12 @@
 
         @pl.when(k == 0)
         def _():
+            x_forward(1)
             y_done(1)
             d_copy(1).start()
-            x_forward(1)
+            for v in (5, 6, 7):
+                b_copy(v).wait_recv()
+                y_start(v)
             for v in (3, 4):
                 z_copy(v).wait_recv()
                 z_copy(v + 2).start()

time: 66.3 us -> 65.4 us (0.986)
  Pallas kernels: 63.1 us -> 62.3 us
    pallas_call x1, Pallas kernels: 63.1 us -> 62.3 us  [body(): pl.pallas_call(multiply, out_shape=jax.ShapeDtypeStruct((8, 144, 128), BF...]
where the time goes in v4:
time: 65.4 us; the launch traced here: 65.3 us
  Pallas kernels  62.3 us (95%)
  local copies, waits for them, and re-layouts  2.98 us (5%)
    pallas_call x1, Pallas kernels, body(): pl.pallas_call(multiply, out_shape=jax.ShapeDtypeStruct((8, 144, 128), BF...  62.3 us

profile of v4, /device:TPU:1, one launch (start us, length us, event | category | flops | bytes accessed | tf_op | source)
XLA Modules:
  0.0 65.3 jit_solution(9642957018391339217)
XLA Ops:
  0.0 0.9 %reshape.10.right_ref = bf16[60,529]{1,0:T(8,128)(2,1)S(1)} reshape(bf16[5,3,4,529]{3,2,1,0:T(4,128)(2,1)} %bitcast.13) | data formatting | bytes 126960 | tf_op jit(solution)/shard_map/reshape | solution.py:410
  0.9 0.0 copy-start
  0.9 0.0 copy-start.1
  1.0 1.1 %reshape.9.left_ref = bf16[192,529]{1,0:T(8,128)(2,1)S(1)} reshape(bf16[48,1,4,529]{3,2,1,0:T(4,128)(2,1)} %param.4) | data formatting | bytes 406272 | tf_op jit(solution)/shard_map/reshape | solution.py:408
  2.0 0.0 copy-done
  2.0 0.0 copy-done.1
  2.1 62.3 %multiply.1 = bf16[8,144,128]{2,1,0:T(8,128)(2,1)S(1)} custom-call(bf16[192,529]{1,0:T(8,128)(2,1)S(1)} %reshape.9.left_ref, s32[4,48]{1,0:T(4,128)S(1)} %bitcast.12, bf16[60,529]{1,0:T(8,128)(2,1)S(1)} %reshape.10.right_ref, s32[3,4,5]{2,1,0:T(4,128)S(1)} %bitcast.11), custom_call_target="tpu_custom_call" | custom-call | tf_op jit(solution)/shard_map/multiply/pallas_call | solution.py:414
  64.3 0.1 reshape.11
  64.4 0.9 %copy.6 = bf16[1104,92]{0,1:T(8,128)(2,1)} copy(bf16[1104,92]{1,0:T(8,128)(2,1)S(1)} %reshape.11) | data formatting | bytes 406272 | tf_op jit(solution)/shard_map/reshape | solution.py:445
Async XLA Ops:
  0.9 1.1 %copy-start = (s32[1,5,4,3]{1,2,3,0:T(4,128)S(1)}, s32[1,5,4,3]{1,2,3,0:T(4,128)}, u32[]{:S(2)}) copy-start(s32[1,5,4,3]{1,2,3,0:T(4,128)} %param.7) | copy-start | bytes 724
  0.9 1.1 %copy-start.1 = (s32[48,1,4]{0,2,1:T(4,128)S(1)}, s32[48,1,4]{0,2,1:T(4,128)}, u32[]{:S(2)}) copy-start(s32[48,1,4]{0,2,1:T(4,128)} %param.5) | copy-start | bytes 2308

commit v5 on v4

--- a/solution.py
+++ b/solution.py
@@ -169,6 +169,9 @@
     j_id = iota((32, 128), 0).astype(F32).astype(BF)
 
     ACC[...] = jnp.zeros_like(ACC)
+    for held in (LDA, LDB):
+        for st in range(2):
+            held[pl.ds(256 * st + 192, 64), :] = jnp.zeros((64, 1024), BF)
     jj = div23(lane)
     cc = lane - 23 * jj
     ni = iota((736, 1), 0)
@@ -215,9 +218,9 @@
                         v = jnp.zeros((16, 128), BF)
                         for s in range(4):
                             v = jnp.where(masks[s][m], slots[s], v)
-                        ld[st, pl.ds(16 * ap, 16), pl.ds(512 * i + 128 * m, 128)] = v
-
-    def take(u, j, ld):
+                        ld[pl.ds(256 * st + 16 * ap, 16), pl.ds(512 * i + 128 * m, 128)] = v
+
+    def dense(u, j):
         tiles = []
         for m in range(8):
             block = RW[u, m % 4, 2 * j + m // 4]
@@ -229,9 +232,10 @@
                     v = jnp.where(masks[s], jnp.broadcast_to(block[24 * s + c : 24 * s + c + 1], (32, 128)), v)
                 rows.append(v)
             tiles.append(jnp.concatenate(rows, axis=0))
-        full = jnp.concatenate(tiles, axis=1)
-        for st in range(2):
-            ACC[st] += lax.dot_general(full, ld[st], (((1,), (1,)), ((), ())), preferred_element_type=F32)
+        return jnp.concatenate(tiles, axis=1)
+
+    def take(u, j, ld):
+        ACC[...] += lax.dot_general(dense(u, j), ld[...], (((1,), (1,)), ((), ())), preferred_element_type=F32)
 
     def x_start(k):
         x_copy(k, 0).start()
@@ -347,20 +351,28 @@
         def _():
             d_copy(k + 1).wait_recv()
 
-        fill(unit(jnp.minimum(k + 1, 7)), 0, LDA)
-        take(u, 1, LDB)
+        @pl.when(k <= 6)
+        def _():
+            fill(unit(k + 1), 0, LDA)
+            take(u, 1, LDB)
+
         return carry
 
     lax.fori_loop(0, 8, step, 0)
-    p_copy = copy(ACC.at[1 - e], OTHER, p_sem.at[0], p_sem.at[1], partner)
+    full = dense(unit(7), 1)
+    theirs = pl.ds(pl.multiple_of(256 * (1 - e), 256), 256)
+    ours = pl.ds(pl.multiple_of(256 * e, 256), 256)
+    ACC[:, theirs] += lax.dot_general(full, LDB[theirs, :], (((1,), (1,)), ((), ())), preferred_element_type=F32)
+    p_copy = copy(ACC.at[:, theirs], OTHER, p_sem.at[0], p_sem.at[1], partner)
     p_copy.start()
+    ACC[:, ours] += lax.dot_general(full, LDB[ours, :], (((1,), (1,)), ((), ())), preferred_element_type=F32)
     p_copy.wait_recv()
 
     mr = iota((144, 1), 0)
     mi = div23(mr)
     ma = mr - 23 * mi
-    rows_pick = onehot(jnp.where(mr < 138, 8 * ma + mi, 9999) == iota((144, 192), 1))
-    res = (ACC[e] + OTHER[...]).astype(BF)
+    rows_pick = onehot(jnp.where(mr < 138, 8 * ma + mi, 9999) == iota((144, 256), 1))
+    res = (ACC[:, ours] + OTHER[...]).astype(BF)
     turned = lax.dot_general(rows_pick, res, (((1,), (1,)), ((), ())), preferred_element_type=F32).astype(BF)
     spread = jnp.dot(turned, GS[...], preferred_element_type=F32).astype(BF)
     for d in range(8):
@@ -421,10 +433,10 @@
             pltpu.VMEM((4, 72, 128), BF),
             pltpu.VMEM((2, 4, 8, 160, 128), BF),
             pltpu.VMEM((8, 4, 4, 72, 128), BF),
-            pltpu.VMEM((2, 192, 1024), BF),
-            pltpu.VMEM((2, 192, 1024), BF),
-            pltpu.VMEM((2, 736, 192), F32),
-            pltpu.VMEM((736, 192), F32),
+            pltpu.VMEM((512, 1024), BF),
+            pltpu.VMEM((512, 1024), BF),
+            pltpu.VMEM((736, 512), F32),
+            pltpu.VMEM((736, 256), F32),
             pltpu.VMEM((736, 1024), BF),
             pltpu.VMEM((8, 144, 128), BF),
             dma((3,)), dma((3,)),

time: 65.4 us -> 65.1 us (level)
  no operation moved by 1% of the time
where the time goes in v5:
time: 65.1 us; the launch traced here: 65 us
  Pallas kernels  62 us (95%)
  local copies, waits for them, and re-layouts  2.98 us (5%)
    pallas_call x1, Pallas kernels, body(): pl.pallas_call(multiply, out_shape=jax.ShapeDtypeStruct((8, 144, 128), BF...  62 us

profile of v5, /device:TPU:1, one launch (start us, length us, event | category | flops | bytes accessed | tf_op | source)
XLA Modules:
  0.0 65.0 jit_solution(7661025248050986557)
XLA Ops:
  0.0 0.9 %reshape.10.right_ref = bf16[60,529]{1,0:T(8,128)(2,1)S(1)} reshape(bf16[5,3,4,529]{3,2,1,0:T(4,128)(2,1)} %bitcast.13) | data formatting | bytes 126960 | tf_op jit(solution)/shard_map/reshape | solution.py:422
  0.9 0.0 copy-start
  0.9 0.0 copy-start.1
  1.0 1.1 %reshape.9.left_ref = bf16[192,529]{1,0:T(8,128)(2,1)S(1)} reshape(bf16[48,1,4,529]{3,2,1,0:T(4,128)(2,1)} %param.4) | data formatting | bytes 406272 | tf_op jit(solution)/shard_map/reshape | solution.py:420
  2.0 0.0 copy-done
  2.0 0.0 copy-done.1
  2.1 62.0 %multiply.1 = bf16[8,144,128]{2,1,0:T(8,128)(2,1)S(1)} custom-call(bf16[192,529]{1,0:T(8,128)(2,1)S(1)} %reshape.9.left_ref, s32[4,48]{1,0:T(4,128)S(1)} %bitcast.12, bf16[60,529]{1,0:T(8,128)(2,1)S(1)} %reshape.10.right_ref, s32[3,4,5]{2,1,0:T(4,128)S(1)} %bitcast.11), custom_call_target="tpu_custom_call" | custom-call | tf_op jit(solution)/shard_map/multiply/pallas_call | solution.py:426
  64.0 0.1 reshape.11
  64.1 0.9 %copy.6 = bf16[1104,92]{0,1:T(8,128)(2,1)} copy(bf16[1104,92]{1,0:T(8,128)(2,1)S(1)} %reshape.11) | data formatting | bytes 406272 | tf_op jit(solution)/shard_map/reshape | solution.py:457
Async XLA Ops:
  0.9 1.1 %copy-start = (s32[1,5,4,3]{1,2,3,0:T(4,128)S(1)}, s32[1,5,4,3]{1,2,3,0:T(4,128)}, u32[]{:S(2)}) copy-start(s32[1,5,4,3]{1,2,3,0:T(4,128)} %param.7) | copy-start | bytes 724
  0.9 1.1 %copy-start.1 = (s32[48,1,4]{0,2,1:T(4,128)S(1)}, s32[48,1,4]{0,2,1:T(4,128)}, u32[]{:S(2)}) copy-start(s32[48,1,4]{0,2,1:T(4,128)} %param.5) | copy-start | bytes 2308

commit v6 on v5

--- a/solution.py
+++ b/solution.py
@@ -339,13 +339,17 @@
             zh_copy(0).wait_recv()
             zh_copy(1).wait_recv()
 
-        @pl.when((k >= 1) & (k <= 5))
+        @pl.when((k >= 1) & (k <= 2))
         def _():
             x_forward(k + 2)
 
         @pl.when((k >= 1) & (k <= 3))
         def _():
             x_start(k + 4)
+
+        @pl.when((k >= 2) & (k <= 4))
+        def _():
+            x_forward(k + 3)
 
         @pl.when(k <= 6)
         def _():

time: 65.1 us -> 68.4 us (1.051)
  Pallas kernels: 62 us -> 65.3 us
    pallas_call x1, Pallas kernels: 62 us -> 65.3 us  [body(): pl.pallas_call(multiply, out_shape=jax.ShapeDtypeStruct((8, 144, 128), BF...]
where the time goes in v6:
time: 68.4 us; the launch traced here: 68.3 us
  Pallas kernels  65.3 us (95%)
  local copies, waits for them, and re-layouts  2.98 us (4%)
    pallas_call x1, Pallas kernels, body(): pl.pallas_call(multiply, out_shape=jax.ShapeDtypeStruct((8, 144, 128), BF...  65.3 us

profile of v6, /device:TPU:1, one launch (start us, length us, event | category | flops | bytes accessed | tf_op | source)
XLA Modules:
  0.0 68.3 jit_solution(14769104414205355493)
XLA Ops:
  0.0 0.9 %reshape.10.right_ref = bf16[60,529]{1,0:T(8,128)(2,1)S(1)} reshape(bf16[5,3,4,529]{3,2,1,0:T(4,128)(2,1)} %bitcast.13) | data formatting | bytes 126960 | tf_op jit(solution)/shard_map/reshape | solution.py:426
  0.9 0.0 copy-start
  0.9 0.0 copy-start.1
  1.0 1.1 %reshape.9.left_ref = bf16[192,529]{1,0:T(8,128)(2,1)S(1)} reshape(bf16[48,1,4,529]{3,2,1,0:T(4,128)(2,1)} %param.4) | data formatting | bytes 406272 | tf_op jit(solution)/shard_map/reshape | solution.py:424
  2.0 0.0 copy-done
  2.0 0.0 copy-done.1
  2.1 65.3 %multiply.1 = bf16[8,144,128]{2,1,0:T(8,128)(2,1)S(1)} custom-call(bf16[192,529]{1,0:T(8,128)(2,1)S(1)} %reshape.9.left_ref, s32[4,48]{1,0:T(4,128)S(1)} %bitcast.12, bf16[60,529]{1,0:T(8,128)(2,1)S(1)} %reshape.10.right_ref, s32[3,4,5]{2,1,0:T(4,128)S(1)} %bitcast.11), custom_call_target="tpu_custom_call" | custom-call | tf_op jit(solution)/shard_map/multiply/pallas_call | solution.py:430
  67.3 0.1 reshape.11
  67.4 0.9 %copy.6 = bf16[1104,92]{0,1:T(8,128)(2,1)} copy(bf16[1104,92]{1,0:T(8,128)(2,1)S(1)} %reshape.11) | data formatting | bytes 406272 | tf_op jit(solution)/shard_map/reshape | solution.py:461
Async XLA Ops:
  0.9 1.1 %copy-start = (s32[1,5,4,3]{1,2,3,0:T(4,128)S(1)}, s32[1,5,4,3]{1,2,3,0:T(4,128)}, u32[]{:S(2)}) copy-start(s32[1,5,4,3]{1,2,3,0:T(4,128)} %param.7) | copy-start | bytes 724
  0.9 1.1 %copy-start.1 = (s32[48,1,4]{0,2,1:T(4,128)S(1)}, s32[48,1,4]{0,2,1:T(4,128)}, u32[]{:S(2)}) copy-start(s32[48,1,4]{0,2,1:T(4,128)} %param.5) | copy-start | bytes 2308
